TPU v7x, 128 devices: a whole 4x4x4 slice. The times are simulated.
128 devices in a mesh: seq: 64 (over z, y, x), tp: 2 (over core).
Axes of the slice: x: 4, y: 4, z: 4, core: 2. Of those that a mesh axis runs over, the one named last changes fastest.
Arguments:
- patches: bfloat16 [16384, 1280], P('seq'), may hold values from -60 to 60
- merge_up: bfloat16 [5120, 2560], P(None, 'tp'), may hold values from -0.078125 to 0.078125
- merge_down: bfloat16 [2560, 3584], P('tp'), may hold values from -0.125 to 0.125
- dest: int32 [4096], P('seq'), may hold values from 0 to 63, as said below
- slot: int32 [4096], P('seq'), may hold values from 0 to 255, as said below
- text: bfloat16 [16384, 3584], P('seq'), may hold values from -60 to 60
- positions: int32 [3, 16384], P(None, 'seq'), may hold values from 0 to 1023
- documents: int32 [16384], P('seq'), may hold values from 0 to 7, never falling along the last dimension, each value on 1 to 8448 neighbouring positions
- w_query: bfloat16 [3584, 1792], P('seq', 'tp'), may hold values from -8 to 8
- w_key: bfloat16 [3584, 256], P('seq', 'tp'), may hold values from -8 to 8
- w_value: bfloat16 [3584, 256], P('seq', 'tp'), may hold values from -0.09375 to 0.09375
Outputs:
- layer_input: bfloat16 [16384, 3584], P('seq', 'tp')
- attended: bfloat16 [16384, 1792], P('seq', 'tp')
Inputs may be any that keep to these rules, and one draw needn't show every extreme that they name: `dest`: the rows of one device name each sequence shard at most 2 times, and in every draw some sequence shard is named 2 times by the rows of every device. `slot`: no two image rows share both a sequence shard and a position. `documents`: document numbers never fall along the tokens.
All inputs are finite; a program needn't handle non-finite values.
Results may differ from a plain program's by a relative error of at most 0.0065.
Values may be sent and summed in bfloat16 or wider, within the bound.
A program may use at most 128 MiB of HBM per device.

v0:
```python
import jax
import jax.numpy as jnp
from jax import lax
from jax.sharding import PartitionSpec as P

HEAD = 128


epsilon = 1e-06
theta_base = 1000000.0
masked_score = -1e30
block_rows = 512


def copy_for_each(x, axis):
    size = lax.axis_size(axis)
    return lax.all_to_all(jnp.broadcast_to(x[None], (size, *x.shape)), axis, 0, 0, tiled=True)


def of_everyone(x, axis):
    everything = copy_for_each(x, axis)
    return jnp.sum(everything, axis=0)


def sent_together(arrays, axis, dim, along):
    ends, at = ([], 0)
    for a in arrays[:-1]:
        at += a.shape[along]
        ends.append(at)
    both = jnp.concatenate(arrays, axis=along)
    return tuple(jnp.split(lax.all_gather(both, axis, axis=dim, tiled=True), ends, axis=along))


def rms_rows(values):
    floats = values.astype(jnp.float32)
    return floats * lax.rsqrt(jnp.mean(floats * floats, axis=-1, keepdims=True) + epsilon)


def rotate(vectors, positions):
    half_dim = vectors.shape[-1] // 2
    first_end = half_dim // 4
    second_end = first_end + 3 * half_dim // 8
    pair_ids = jnp.arange(half_dim, dtype=jnp.int32)
    inverse = jnp.power(theta_base, -2.0 * pair_ids.astype(jnp.float32) / (2 * half_dim))
    coords = positions.astype(jnp.float32)
    chosen = jnp.where(
        pair_ids[None, :] < first_end,
        coords[0][:, None],
        jnp.where(pair_ids[None, :] < second_end, coords[1][:, None], coords[2][:, None]),
    )
    angles = chosen * inverse[None, :]
    cosine = jnp.cos(angles)[:, None, :]
    sine = jnp.sin(angles)[:, None, :]
    lower_part = vectors[..., :half_dim]
    upper_part = vectors[..., half_dim:]
    return jnp.concatenate(
        [lower_part * cosine - upper_part * sine, upper_part * cosine + lower_part * sine], axis=-1
    )


def attend(
    carry, queries, key_block, value_block, doc_block, key_first, query_pos, query_doc, score_scale
):
    maxima, totals, summed = carry
    scores = (
        jnp.einsum("qkgd,pkd->kgqp", queries, key_block, preferred_element_type=jnp.float32)
        * score_scale
    )
    key_pos = key_first + jnp.arange(key_block.shape[0], dtype=jnp.int32)
    allowed = (query_pos[:, None] >= key_pos[None, :]) & (query_doc[:, None] == doc_block[None, :])
    scores = jnp.where(allowed, scores, masked_score)
    new_max = jnp.maximum(maxima, jnp.max(scores, axis=-1))
    weights = jnp.where(allowed, jnp.exp(scores - new_max[..., None]), 0.0)
    factor = jnp.exp(maxima - new_max)
    totals = totals * factor + jnp.sum(weights, axis=-1)
    summed = summed * factor[..., None] + jnp.einsum(
        "kgqp,pkd->kgqd",
        weights.astype(jnp.bfloat16),
        value_block,
        preferred_element_type=jnp.float32,
    )
    return (new_max, totals, summed)


def per_device(
    patches, merge_up, merge_down, dest, slot, text, positions, documents, w_query, w_key, w_value
):
    seq_count = lax.axis_size("seq")
    tp_count = lax.axis_size("tp")
    tok_dev = text.shape[0]
    model_width = text.shape[1]
    img_dev = dest.shape[0]
    capacity = max(2, 2 * img_dev // seq_count)
    grouped = rms_rows(patches).astype(jnp.bfloat16).reshape(img_dev, -1)
    merger_hidden = jax.nn.gelu(
        jnp.dot(grouped, merge_up, preferred_element_type=jnp.float32), approximate=False
    ).astype(jnp.bfloat16)
    partial_sums = jnp.dot(merger_hidden, merge_down, preferred_element_type=jnp.float32)
    same_dest = dest[:, None] == dest[None, :]
    earlier = jnp.arange(img_dev)[:, None] > jnp.arange(img_dev)[None, :]
    slot_order = jnp.sum(same_dest & earlier, axis=1)
    send_place = dest * capacity + slot_order
    slot_buffer = jnp.full((seq_count * capacity,), tok_dev, jnp.int32).at[send_place].set(slot)
    slot_buffer = slot_buffer.reshape(seq_count, capacity)
    share_width = model_width // tp_count
    own_part = lax.axis_index("tp")
    merged = of_everyone(partial_sums, "tp").astype(jnp.bfloat16)
    buffer = jnp.zeros((seq_count * capacity, model_width), jnp.bfloat16).at[send_place].set(merged)
    buffer = buffer.reshape(seq_count, capacity, model_width)
    arrived, places = (
        lax.all_to_all(buffer, "seq", split_axis=0, concat_axis=0, tiled=True),
        lax.all_to_all(slot_buffer, "seq", split_axis=0, concat_axis=0, tiled=True),
    )
    layer_input = text.at[places.reshape(-1)].set(arrived.reshape(-1, model_width), mode="drop")
    layer_part = lax.dynamic_slice_in_dim(layer_input, own_part * share_width, share_width, 1)
    normed = rms_rows(layer_input).astype(jnp.bfloat16)
    pieces = sent_together((w_query, w_key, w_value), "seq", 0, 1)
    query_raw = jnp.dot(normed, pieces[0], preferred_element_type=jnp.float32)
    key_raw = jnp.dot(normed, pieces[1], preferred_element_type=jnp.float32)
    value_raw = jnp.dot(normed, pieces[2], preferred_element_type=jnp.float32)
    kv_local = w_key.shape[1] // HEAD
    group_size = w_query.shape[1] // w_key.shape[1]
    roped_query = rotate(query_raw.reshape(tok_dev, -1, HEAD), positions).astype(jnp.bfloat16)
    roped_query = roped_query.reshape(tok_dev, kv_local, group_size, HEAD)
    roped_key = rotate(key_raw.reshape(tok_dev, kv_local, HEAD), positions).astype(jnp.bfloat16)
    values = value_raw.reshape(tok_dev, kv_local, HEAD).astype(jnp.bfloat16)
    own_index = lax.axis_index("seq")
    queries = roped_query
    query_pos = own_index * tok_dev + jnp.arange(tok_dev, dtype=jnp.int32)
    last_query = jnp.max(query_pos)
    first_doc = jnp.min(documents)
    score_scale = HEAD ** (-0.5)

    def visit(carry, key_block, value_block, doc_block, key_first):
        unused = (key_first > last_query) | (doc_block[-1] < first_doc)
        return lax.cond(
            unused,
            lambda current: current,
            lambda current: attend(
                current,
                queries,
                key_block,
                value_block,
                doc_block,
                key_first,
                query_pos,
                documents,
                score_scale,
            ),
            carry,
        )

    initial = (
        jnp.full((kv_local, group_size, tok_dev), masked_score, jnp.float32),
        jnp.zeros((kv_local, group_size, tok_dev), jnp.float32),
        jnp.zeros((kv_local, group_size, tok_dev, HEAD), jnp.float32),
    )
    key_piece = lax.all_gather(roped_key, "seq", axis=0, tiled=True)
    value_piece = lax.all_gather(values, "seq", axis=0, tiled=True)
    doc_piece = lax.all_gather(documents, "seq", axis=0, tiled=True)
    piece_rows = key_piece.shape[0]
    block_count = piece_rows // block_rows
    stacked = (
        key_piece.reshape(block_count, block_rows, kv_local, HEAD),
        value_piece.reshape(block_count, block_rows, kv_local, HEAD),
        doc_piece.reshape(block_count, block_rows),
        jnp.arange(block_count, dtype=jnp.int32),
    )

    def through(current, parts):
        return (visit(current, parts[0], parts[1], parts[2], parts[3] * block_rows), None)

    finished, ignored = lax.scan(through, initial, stacked)
    maxima, totals, summed = finished
    attended = (
        (summed / totals[..., None]).transpose(2, 0, 1, 3).reshape(tok_dev, -1).astype(jnp.bfloat16)
    )
    return (layer_part, attended)


def solution(mesh):
    in_specs = (
        P("seq", None),
        P(None, "tp"),
        P("tp", None),
        P("seq"),
        P("seq"),
        P("seq", None),
        P(None, "seq"),
        P("seq"),
        P("seq", "tp"),
        P("seq", "tp"),
        P("seq", "tp"),
    )
    out_specs = (P("seq", "tp"), P("seq", "tp"))
    return jax.shard_map(
        per_device, mesh=mesh, in_specs=in_specs, out_specs=out_specs, check_vma=False
    )
```

profile of v0, /device:TPU:64, one launch (start us, length us, event | category | flops | bytes accessed | tf_op | source)
XLA Modules:
  0.0 485.6 jit_solution(3593981710146801849)
XLA Ops:
  9.7 12.3 %fusion.50 = f32[64,3584]{1,0:T(8,128)S(1)} fusion(bf16[1280,3584]{1,0:T(8,128)(2,1)} %param.17, bf16[64,5120]{1,0:T(8,128)(2,1)S(1)} %reshape.556, bf16[5120,1280]{1,0:T(8,128)(2,1)} %param.16), kind=kOutput, calls=%fused_computation.75 | convolution fusion | flops 1431388160 | bytes 23855104 | tf_op jit(solution)/shard_map/dot_general | solution.py:98
  29.8 10.7 %all-to-all-start = ((s32[64,1,2]{2,1,0:T(1,128)}), s32[64,1,2]{2,1,0:T(1,128)S(1)}, u32[]{:S(2)}, u32[]{:S(2)}) async-start(s32[64,1,2]{2,1,0:T(1,128)} %bitcast.14), calls=%async_computation | async-start | bytes 65536 | tf_op jit(solution)/shard_map/all_to_all | solution.py:112
  48.2 7.4 %all-to-all-start.2 = ((bf16[64,2,3584]{2,1,0:T(2,128)(2,1)}), bf16[64,2,3584]{2,1,0:T(2,128)(2,1)S(1)}, u32[]{:S(2)}, u32[]{:S(2)}) async-start(bf16[64,2,3584]{2,1,0:T(2,128)(2,1)} %reshape.557), calls=%async_computation.2 | async-start | bytes 1835008 | tf_op jit(solution)/shard_map/all_to_all | solution.py:111
  57.0 13.3 %all-to-all-done.2 = bf16[64,2,3584]{2,1,0:T(2,128)(2,1)S(1)} async-done(((bf16[64,2,3584]{2,1,0:T(2,128)(2,1)}), bf16[64,2,3584]{2,1,0:T(2,128)(2,1)S(1)}, u32[]{:S(2)}, u32[]{:S(2)}) %all-to-all-start.2) | async-done | bytes 917536 | tf_op jit(solution)/shard_map/all_to_all | solution.py:111
  75.7 16.5 %all-gather.6.cloned.1.call-done = bf16[3584,1152]{1,0:T(8,128)(2,1)} async-done(((bf16[56,1152]{1,0:T(8,128)(2,1)}), bf16[3584,1152]{1,0:T(8,128)(2,1)}) %all-gather.6.cloned.1.call-update) | async-done | bytes 8257552 | tf_op jit(solution)/shard_map/all_gather | solution.py:31
  99.2 153.0 %all-gather.1 = s32[64,1,256]{2,1,0:T(1,128)S(1)} all-gather(s32[1,1,256]{2,1,0:T(1,128)S(1)} %bitcast.97), channel_id=1, replica_groups=mesh['seq'=64,'tp'=2] {'seq'}, dimensions={0}, use_global_device_ids=true | all-gather | bytes 66560 | tf_op jit(solution)/shard_map/all_gather | solution.py:160
  253.7 5.5 %fusion.27 = f32[256,896]{0,1:T(8,128)S(1)} fusion(bf16[3584,1152]{1,0:T(8,128)(2,1)} %all-gather.6.cloned.1.call-done, bf16[256,3584]{1,0:T(8,128)(2,1)S(1)} %scatter_fusion, f32[256]{0:T(256)S(1)} %add_rsqrt_fusion), kind=kOutput, calls=%fused_computation.33 | convolution fusion | flops 1646919680 | bytes 9176064 | tf_op jit(solution)/shard_map/dot_general | solution.py:118
  259.7 6.4 %copy.44 = bf16[16384,1,128]{2,0,1:T(8,128)(2,1)} copy(bf16[16384,1,128]{0,2,1:T(8,128)(2,1)} %all-gather.8.cloned.1.call-done) | data formatting | bytes 8388608
  266.2 211.5 %while.15 = (s32[]{:T(128)}, f32[1,7,256]{2,1,0:T(8,128)S(1)}, f32[1,7,256]{2,1,0:T(8,128)S(1)}, f32[1,7,256,128]{3,2,1,0:T(8,128)S(1)}, s32[32]{0:T(128)S(1)}, ...) while((s32[]{:T(128)}, f32[1,7,256]{2,1,0:T(8,128)S(1)}, ...), condition=%wide.region_14.15_spmd.clone, body=%wide.region_9.14_spmd.clone.sunk | while | flops 482547712 | bytes 14221707 | solution.py:173
  279.0 5.2 %conditional.3 = (f32[1,7,256]{2,1,0:T(8,128)S(1)}, f32[1,7,256]{2,1,0:T(8,128)S(1)}, f32[1,7,256,128]{3,2,1,0:T(8,128)S(1)}) conditional(s32[]{:T(128)} %convert_element_type.127, (s32[]{:T(128)}, s32[]{:T(128)}, s32[256]{0:T(256)S(1)}, s32[1,512]{1,0:T(1,128)S(1)}, bf16[32,512,1,128]{3,1,2,0:T(8,128)(2,1)}, /*index=5*/s32[]{:T(128)}, ...), branch_computations={%region_10.12_spmd, %region_13.13_spmd} | conditional | flops 482547712 | bytes 14201888 | solution.py:136
  288.0 5.2 %conditional.3 = (f32[1,7,256]{2,1,0:T(8,128)S(1)}, f32[1,7,256]{2,1,0:T(8,128)S(1)}, f32[1,7,256,128]{3,2,1,0:T(8,128)S(1)}) conditional(s32[]{:T(128)} %convert_element_type.127, (s32[]{:T(128)}, s32[]{:T(128)}, s32[256]{0:T(256)S(1)}, s32[1,512]{1,0:T(1,128)S(1)}, bf16[32,512,1,128]{3,1,2,0:T(8,128)(2,1)}, /*index=5*/s32[]{:T(128)}, ...), branch_computations={%region_10.12_spmd, %region_13.13_spmd} | conditional | flops 482547712 | bytes 14201888 | solution.py:136
  297.0 5.2 %conditional.3 = (f32[1,7,256]{2,1,0:T(8,128)S(1)}, f32[1,7,256]{2,1,0:T(8,128)S(1)}, f32[1,7,256,128]{3,2,1,0:T(8,128)S(1)}) conditional(s32[]{:T(128)} %convert_element_type.127, (s32[]{:T(128)}, s32[]{:T(128)}, s32[256]{0:T(256)S(1)}, s32[1,512]{1,0:T(1,128)S(1)}, bf16[32,512,1,128]{3,1,2,0:T(8,128)(2,1)}, /*index=5*/s32[]{:T(128)}, ...), branch_computations={%region_10.12_spmd, %region_13.13_spmd} | conditional | flops 482547712 | bytes 14201888 | solution.py:136
  306.0 5.2 %conditional.3 = (f32[1,7,256]{2,1,0:T(8,128)S(1)}, f32[1,7,256]{2,1,0:T(8,128)S(1)}, f32[1,7,256,128]{3,2,1,0:T(8,128)S(1)}) conditional(s32[]{:T(128)} %convert_element_type.127, (s32[]{:T(128)}, s32[]{:T(128)}, s32[256]{0:T(256)S(1)}, s32[1,512]{1,0:T(1,128)S(1)}, bf16[32,512,1,128]{3,1,2,0:T(8,128)(2,1)}, /*index=5*/s32[]{:T(128)}, ...), branch_computations={%region_10.12_spmd, %region_13.13_spmd} | conditional | flops 482547712 | bytes 14201888 | solution.py:136
  315.1 5.2 %conditional.3 = (f32[1,7,256]{2,1,0:T(8,128)S(1)}, f32[1,7,256]{2,1,0:T(8,128)S(1)}, f32[1,7,256,128]{3,2,1,0:T(8,128)S(1)}) conditional(s32[]{:T(128)} %convert_element_type.127, (s32[]{:T(128)}, s32[]{:T(128)}, s32[256]{0:T(256)S(1)}, s32[1,512]{1,0:T(1,128)S(1)}, bf16[32,512,1,128]{3,1,2,0:T(8,128)(2,1)}, /*index=5*/s32[]{:T(128)}, ...), branch_computations={%region_10.12_spmd, %region_13.13_spmd} | conditional | flops 482547712 | bytes 14201888 | solution.py:136
  324.1 5.2 %conditional.3 = (f32[1,7,256]{2,1,0:T(8,128)S(1)}, f32[1,7,256]{2,1,0:T(8,128)S(1)}, f32[1,7,256,128]{3,2,1,0:T(8,128)S(1)}) conditional(s32[]{:T(128)} %convert_element_type.127, (s32[]{:T(128)}, s32[]{:T(128)}, s32[256]{0:T(256)S(1)}, s32[1,512]{1,0:T(1,128)S(1)}, bf16[32,512,1,128]{3,1,2,0:T(8,128)(2,1)}, /*index=5*/s32[]{:T(128)}, ...), branch_computations={%region_10.12_spmd, %region_13.13_spmd} | conditional | flops 482547712 | bytes 14201888 | solution.py:136
  333.1 5.2 %conditional.3 = (f32[1,7,256]{2,1,0:T(8,128)S(1)}, f32[1,7,256]{2,1,0:T(8,128)S(1)}, f32[1,7,256,128]{3,2,1,0:T(8,128)S(1)}) conditional(s32[]{:T(128)} %convert_element_type.127, (s32[]{:T(128)}, s32[]{:T(128)}, s32[256]{0:T(256)S(1)}, s32[1,512]{1,0:T(1,128)S(1)}, bf16[32,512,1,128]{3,1,2,0:T(8,128)(2,1)}, /*index=5*/s32[]{:T(128)}, ...), branch_computations={%region_10.12_spmd, %region_13.13_spmd} | conditional | flops 482547712 | bytes 14201888 | solution.py:136
  342.1 5.2 %conditional.3 = (f32[1,7,256]{2,1,0:T(8,128)S(1)}, f32[1,7,256]{2,1,0:T(8,128)S(1)}, f32[1,7,256,128]{3,2,1,0:T(8,128)S(1)}) conditional(s32[]{:T(128)} %convert_element_type.127, (s32[]{:T(128)}, s32[]{:T(128)}, s32[256]{0:T(256)S(1)}, s32[1,512]{1,0:T(1,128)S(1)}, bf16[32,512,1,128]{3,1,2,0:T(8,128)(2,1)}, /*index=5*/s32[]{:T(128)}, ...), branch_computations={%region_10.12_spmd, %region_13.13_spmd} | conditional | flops 482547712 | bytes 14201888 | solution.py:136
  351.1 5.2 %conditional.3 = (f32[1,7,256]{2,1,0:T(8,128)S(1)}, f32[1,7,256]{2,1,0:T(8,128)S(1)}, f32[1,7,256,128]{3,2,1,0:T(8,128)S(1)}) conditional(s32[]{:T(128)} %convert_element_type.127, (s32[]{:T(128)}, s32[]{:T(128)}, s32[256]{0:T(256)S(1)}, s32[1,512]{1,0:T(1,128)S(1)}, bf16[32,512,1,128]{3,1,2,0:T(8,128)(2,1)}, /*index=5*/s32[]{:T(128)}, ...), branch_computations={%region_10.12_spmd, %region_13.13_spmd} | conditional | flops 482547712 | bytes 14201888 | solution.py:136
  360.1 5.2 %conditional.3 = (f32[1,7,256]{2,1,0:T(8,128)S(1)}, f32[1,7,256]{2,1,0:T(8,128)S(1)}, f32[1,7,256,128]{3,2,1,0:T(8,128)S(1)}) conditional(s32[]{:T(128)} %convert_element_type.127, (s32[]{:T(128)}, s32[]{:T(128)}, s32[256]{0:T(256)S(1)}, s32[1,512]{1,0:T(1,128)S(1)}, bf16[32,512,1,128]{3,1,2,0:T(8,128)(2,1)}, /*index=5*/s32[]{:T(128)}, ...), branch_computations={%region_10.12_spmd, %region_13.13_spmd} | conditional | flops 482547712 | bytes 14201888 | solution.py:136
  369.2 5.2 %conditional.3 = (f32[1,7,256]{2,1,0:T(8,128)S(1)}, f32[1,7,256]{2,1,0:T(8,128)S(1)}, f32[1,7,256,128]{3,2,1,0:T(8,128)S(1)}) conditional(s32[]{:T(128)} %convert_element_type.127, (s32[]{:T(128)}, s32[]{:T(128)}, s32[256]{0:T(256)S(1)}, s32[1,512]{1,0:T(1,128)S(1)}, bf16[32,512,1,128]{3,1,2,0:T(8,128)(2,1)}, /*index=5*/s32[]{:T(128)}, ...), branch_computations={%region_10.12_spmd, %region_13.13_spmd} | conditional | flops 482547712 | bytes 14201888 | solution.py:136
  378.2 5.2 %conditional.3 = (f32[1,7,256]{2,1,0:T(8,128)S(1)}, f32[1,7,256]{2,1,0:T(8,128)S(1)}, f32[1,7,256,128]{3,2,1,0:T(8,128)S(1)}) conditional(s32[]{:T(128)} %convert_element_type.127, (s32[]{:T(128)}, s32[]{:T(128)}, s32[256]{0:T(256)S(1)}, s32[1,512]{1,0:T(1,128)S(1)}, bf16[32,512,1,128]{3,1,2,0:T(8,128)(2,1)}, /*index=5*/s32[]{:T(128)}, ...), branch_computations={%region_10.12_spmd, %region_13.13_spmd} | conditional | flops 482547712 | bytes 14201888 | solution.py:136
  387.2 5.2 %conditional.3 = (f32[1,7,256]{2,1,0:T(8,128)S(1)}, f32[1,7,256]{2,1,0:T(8,128)S(1)}, f32[1,7,256,128]{3,2,1,0:T(8,128)S(1)}) conditional(s32[]{:T(128)} %convert_element_type.127, (s32[]{:T(128)}, s32[]{:T(128)}, s32[256]{0:T(256)S(1)}, s32[1,512]{1,0:T(1,128)S(1)}, bf16[32,512,1,128]{3,1,2,0:T(8,128)(2,1)}, /*index=5*/s32[]{:T(128)}, ...), branch_computations={%region_10.12_spmd, %region_13.13_spmd} | conditional | flops 482547712 | bytes 14201888 | solution.py:136
  396.2 5.2 %conditional.3 = (f32[1,7,256]{2,1,0:T(8,128)S(1)}, f32[1,7,256]{2,1,0:T(8,128)S(1)}, f32[1,7,256,128]{3,2,1,0:T(8,128)S(1)}) conditional(s32[]{:T(128)} %convert_element_type.127, (s32[]{:T(128)}, s32[]{:T(128)}, s32[256]{0:T(256)S(1)}, s32[1,512]{1,0:T(1,128)S(1)}, bf16[32,512,1,128]{3,1,2,0:T(8,128)(2,1)}, /*index=5*/s32[]{:T(128)}, ...), branch_computations={%region_10.12_spmd, %region_13.13_spmd} | conditional | flops 482547712 | bytes 14201888 | solution.py:136
  414.2 5.2 %conditional.3 = (f32[1,7,256]{2,1,0:T(8,128)S(1)}, f32[1,7,256]{2,1,0:T(8,128)S(1)}, f32[1,7,256,128]{3,2,1,0:T(8,128)S(1)}) conditional(s32[]{:T(128)} %convert_element_type.127, (s32[]{:T(128)}, s32[]{:T(128)}, s32[256]{0:T(256)S(1)}, s32[1,512]{1,0:T(1,128)S(1)}, bf16[32,512,1,128]{3,1,2,0:T(8,128)(2,1)}, /*index=5*/s32[]{:T(128)}, ...), branch_computations={%region_10.12_spmd, %region_13.13_spmd} | conditional | flops 482547712 | bytes 14201888 | solution.py:136
  (400 shorter events, 171.9 us)
Async XLA Ops:
  7.2 1.7 copy-start.1
  7.2 1.0 copy-start.2
  7.2 1.0 copy-start.5
  7.2 0.9 copy-start.4
  7.2 85.0 %all-gather.6.cloned.1.call-start = ((), (), s32[]{:S(2)}) async-start(), calls=%async_computation.3 | async-start | bytes 8386560 | tf_op jit(solution)/shard_map/all_gather | solution.py:31
  21.9 5.3 %copy-start.7 = (s32[64]{0:T(128)S(1)}, s32[64]{0:T(128)}, u32[]{:S(2)}) copy-start(s32[64]{0:T(128)} %param.18) | copy-start | bytes 772
  23.4 6.4 %all-to-all-start.1 = ((f32[2,64,3584]{2,1,0:T(8,128)}), f32[2,64,3584]{2,1,0:T(8,128)S(1)}, u32[]{:S(2)}, u32[]{:S(2)}) async-start(f32[2,64,3584]{2,1,0:T(8,128)} %broadcast_in_dim.137), calls=%async_computation.1 | async-start | bytes 3670016 | tf_op jit(solution)/shard_map/all_to_all | solution.py:17
  29.8 18.4 %all-to-all-start = ((s32[64,1,2]{2,1,0:T(1,128)}), s32[64,1,2]{2,1,0:T(1,128)S(1)}, u32[]{:S(2)}, u32[]{:S(2)}) async-start(s32[64,1,2]{2,1,0:T(1,128)} %bitcast.14), calls=%async_computation | async-start | bytes 65536 | tf_op jit(solution)/shard_map/all_to_all | solution.py:112
  40.6 15.1 %copy-start.6 = (s32[3,256]{1,0:T(4,128)S(1)}, s32[3,256]{1,0:T(4,128)}, u32[]{:S(2)}) copy-start(s32[3,256]{1,0:T(4,128)} %param.21) | copy-start | bytes 9220
  41.7 29.9 %copy-start = (bf16[256,3584]{1,0:T(8,128)(2,1)S(1)}, bf16[256,3584]{1,0:T(8,128)(2,1)}, u32[]{:S(2)}) copy-start(bf16[256,3584]{1,0:T(8,128)(2,1)} %param.20) | copy-start | bytes 5505028
  48.2 22.1 %all-to-all-start.2 = ((bf16[64,2,3584]{2,1,0:T(2,128)(2,1)}), bf16[64,2,3584]{2,1,0:T(2,128)(2,1)S(1)}, u32[]{:S(2)}, u32[]{:S(2)}) async-start(bf16[64,2,3584]{2,1,0:T(2,128)(2,1)} %reshape.557), calls=%async_computation.2 | async-start | bytes 1835008 | tf_op jit(solution)/shard_map/all_to_all | solution.py:111
  55.6 204.1 %all-gather.8.cloned.1.call-start = ((), (), s32[]{:S(2)}) async-start(), calls=%async_computation.4 | async-start | bytes 4259840 | tf_op jit(solution)/shard_map/all_gather | solution.py:158
  75.7 22.8 %copy-start.3 = (s32[256]{0:T(256)S(1)}, s32[256]{0:T(256)}, u32[]{:S(2)}) copy-start(s32[256]{0:T(256)} %param.22) | copy-start | bytes 3076
  95.2 170.8 %all-gather.10.cloned.1.call-start = ((), (), s32[]{:S(2)}) async-start(), calls=%async_computation.5 | async-start | bytes 4259840 | tf_op jit(solution)/shard_map/all_gather | solution.py:159
Sparse Core Ops, SparseCore 0:
  11.5 80.7 all-gather.5
  95.5 73.1 all-gather.7
  171.6 68.1 all-gather.9
where the time goes:
time: 485 us; the launch traced here: 486 us
  blocking collectives  153 us (32%)
  matrix products  89.5 us (18%)
  loops' own time  85.4 us (18%)
  local copies, waits for them, and re-layouts  60 us (12%)
  waiting for transfers between devices  33.6 us (7%)
  other arithmetic  28.1 us (6%)
  starting transfers between devices  21.9 us (5%)
  between operations  14 us (3%)
    all_gather x1, blocking collectives, per_device(): doc_piece = lax.all_gather(documents, 'seq', axis=0, tiled=True)  153 us
    another operation x1, loops' own time, per_device(): finished, ignored = lax.scan(through, initial, stacked)  83.7 us
    dot_general x17, matrix products, attend(): jnp.einsum('kgqp,pkd->kgqd', weights.astype(jnp.bfloat16), value_block, p...  39.7 us
    dot_general x17, matrix products, attend(): jnp.einsum('qkgd,pkd->kgqp', queries, key_block, preferred_element_type=j...  27.6 us
    dynamic_slice x64, local copies, waits for them, and re-layouts, per_device(): finished, ignored = lax.scan(through, initial, stacked)  20.2 us
    slice x32, local copies, waits for them, and re-layouts, visit(): unused = (key_first > last_query) | (doc_block[-1] < first_doc)  19.2 us
    all_gather x1, waiting for transfers between devices, sent_together(): lax.all_gather(both, axis, axis=dim, tiled=True)  16.5 us
    reduce_sum x17, other arithmetic, attend(): totals = totals * factor + jnp.sum(weights, axis=-1)  15.2 us
  transfers between devices with their start and end apart: 6, of which 4 were waited for; matrix products, arithmetic and copies ran while one was open for 9% of the time, Pallas kernels for 0%

commit v1 on v0

v1 whole, which is shorter than its diff:
```python
import functools

import jax
import jax.numpy as jnp
from jax import lax
from jax.experimental import pallas as pl
from jax.experimental.pallas import tpu as pltpu
from jax.sharding import PartitionSpec as P

HEAD = 128
EPS = 1e-06
THETA = 1000000.0
MASKED = -1e30
MESH = pl.DeviceIdType.MESH
F32 = jnp.float32
BF16 = jnp.bfloat16
WINDOW = 33


def coords():
    seq = lax.axis_index("seq")
    return (seq // 16, (seq // 4) % 4, seq % 4), lax.axis_index("tp"), seq


def device(zyx, tp):
    return (zyx[0] * 16 + zyx[1] * 4 + zyx[2], tp)


def moved(zyx, dim, by):
    out = list(zyx)
    out[dim] = lax.rem(out[dim] + by + 4, 4)
    return tuple(out)


class Gather:
    def __init__(self, view, send, recv, zyx, tp):
        self.view, self.send, self.recv, self.zyx, self.tp = view, send, recv, zyx, tp
        self.orders = ((2, 1, 0), (1, 0, 2), (0, 2, 1))

    def block(self, part, phase, at, half):
        order = self.orders[part]
        index = [None, None, None]
        for place, dim in enumerate(order):
            if place < phase:
                index[dim] = pl.ds(0, 4)
            elif place == phase:
                index[dim] = at
            else:
                index[dim] = self.zyx[dim]
        if half is not None:
            dim = order[phase - 1]
            index[dim] = pl.ds(2 * half, 2)
        return self.view(part, tuple(index))

    def copy(self, part, phase, kind, incoming=False):
        dim = self.orders[part][phase]
        me = self.zyx[dim]
        up = kind < 3
        back, half = ((0, 0), (0, 1), (1, 0), (0, 1), (0, 0), (1, 1))[kind]
        if phase == 0:
            half = None
        sign = 1 if up else -1
        shift = -sign * (back + (1 if incoming else 0))
        at = lax.rem(me + shift + 4, 4)
        ref = self.block(part, phase, at, half)
        sem = (part * 3 + phase) * 6 + kind
        return pltpu.make_async_remote_copy(
            src_ref=ref,
            dst_ref=ref,
            send_sem=self.send.at[sem],
            recv_sem=self.recv.at[sem],
            device_id=device(moved(self.zyx, dim, sign), self.tp),
            device_id_type=MESH,
        )

    def kinds(self, phase):
        return (0, 3) if phase == 0 else (0, 3, 1, 4)

    def start(self, phase):
        for kind in self.kinds(phase):
            for part in range(3):
                self.copy(part, phase, kind).start()

    def forward(self, phase):
        for part in range(3):
            self.copy(part, phase, 0, True).wait_recv()
            self.copy(part, phase, 2).start()
        if phase:
            for part in range(3):
                self.copy(part, phase, 3, True).wait_recv()
                self.copy(part, phase, 5).start()

    def finish(self, phase):
        rest = (3, 2) if phase == 0 else (1, 4, 2, 5)
        for part in range(3):
            for kind in rest:
                self.copy(part, phase, kind, True).wait_recv()

    def drain(self):
        for phase in range(3):
            for part in range(3):
                for kind in (0, 3, 2) if phase == 0 else range(6):
                    self.copy(part, phase, kind).wait_send()


def iota(shape, dim):
    return lax.broadcasted_iota(jnp.int32, shape, dim)


def to_column(row):
    n = row.shape[1]
    eye = iota((n, n), 0) == iota((n, n), 1)
    return jnp.sum(jnp.where(eye, jnp.broadcast_to(row, (n, n)), 0.0), axis=1, keepdims=True)


def to_row(column):
    n = column.shape[0]
    eye = iota((n, n), 0) == iota((n, n), 1)
    return jnp.sum(jnp.where(eye, jnp.broadcast_to(column, (n, n)), 0.0), axis=0, keepdims=True)


def one_hot(flag):
    return jnp.where(flag, 1.0, 0.0).astype(BF16)


def dot(a, b):
    return jnp.dot(a, b, preferred_element_type=F32)


def front(
    patches, merge_up, merge_down, dest, slot, text, positions, documents, w_query, w_key, w_value,
    layer_out, q_out, kv_out, start_out,
    patch_v, up_v, down_v, text_v, pn, acc, disp, stage1, turned, stage2, part_f, part_s, part_r,
    merged, normed, weights, qkv,
    load, send, recv, send1, recv1, send2, recv2, send3, recv3,
):
    zyx, tp, seq = coords()
    z, y, x = zyx
    own = weights.at[z, y, x]
    loads = [
        pltpu.make_async_copy(w_query, own.at[:, pl.ds(0, 896)], load.at[0]),
        pltpu.make_async_copy(w_key, own.at[:, pl.ds(896, 128)], load.at[1]),
        pltpu.make_async_copy(w_value, own.at[:, pl.ds(1024, 128)], load.at[2]),
        pltpu.make_async_copy(patches, patch_v, load.at[3]),
    ]
    loads += [
        pltpu.make_async_copy(merge_up.at[pl.ds(1280 * p, 1280)], up_v.at[p], load.at[4 + p])
        for p in range(4)
    ]
    loads.append(pltpu.make_async_copy(merge_down, down_v, load.at[8]))
    loads.append(pltpu.make_async_copy(text, text_v, load.at[9]))
    for copy in loads:
        copy.start()

    barrier = pltpu.get_barrier_semaphore()
    partners = []
    for g in range(1, 16):
        partners.append(device(moved(moved(zyx, 0, g // 4), 1, g % 4), tp))
    for g in range(1, 4):
        partners.append(device(moved(zyx, 2, g), tp))
    partners.append((seq, 1 - tp))
    for partner in partners:
        pl.semaphore_signal(barrier, inc=1, device_id=partner, device_id_type=MESH)
    for copy in loads[:3]:
        copy.wait()
    pl.semaphore_wait(barrier, len(partners))

    def part_of(part, index):
        return weights.at[index + (slice(None), pl.ds(384 * part, 384))]

    gather = Gather(part_of, send, recv, zyx, tp)
    gather.start(0)

    loads[3].wait()
    rows = patch_v[...].astype(F32)
    scale = lax.rsqrt(jnp.mean(rows * rows, axis=1, keepdims=True) + EPS)
    scaled = (rows * scale).astype(BF16)
    o, i = iota((256, 256), 0), iota((256, 256), 1)
    pn[...] = dot(one_hot(i == 4 * (o % 64) + o // 64), scaled).astype(BF16)

    gather.forward(0)
    loads[4].wait()
    acc[...] = dot(pn[0:64], up_v[0])
    gather.finish(0)
    gather.start(1)
    for p in range(1, 4):
        loads[4 + p].wait()
        acc[...] += dot(pn[64 * p : 64 * p + 64], up_v[p])
    gather.forward(1)

    h = acc[...]
    hidden = (0.5 * h * (1.0 + lax.erf(h * 0.7071067811865476))).astype(BF16)

    dest_row = dest[...].astype(F32)
    dest_col = to_column(dest_row)
    before = (iota((64, 64), 0) < iota((64, 64), 1)) & (dest_col == dest_row)
    order = jnp.sum(jnp.where(before, 1.0, 0.0), axis=0, keepdims=True)
    place = dest_row * 2.0 + order
    chosen = one_hot(iota((128, 64), 0).astype(F32) == place)
    slot_col = to_column(slot[...].astype(F32)) + 1.0
    lane = iota((64, 128), 1)
    meta = jnp.where(lane == 0, slot_col, 0.0).astype(BF16)
    doc_col = to_column(documents[...].astype(F32))
    doc_lane = (iota((256, 128), 1) - 1).astype(F32)
    counts = jnp.sum(jnp.where(doc_col == doc_lane, 1.0, 0.0), axis=0, keepdims=True)
    routed = dot(chosen, hidden).astype(BF16)
    disp[:, :, 0:1280] = routed.reshape(16, 8, 1280)
    routed_meta = (dot(chosen, meta) + counts).astype(BF16)
    disp[:, :, 1280:1408] = routed_meta.reshape(16, 8, 128)

    me_g = z * 4 + y

    def first(g, incoming):
        away = ((4 - g // 4) % 4 * 4 + (4 - g % 4) % 4) if incoming else g
        far = moved(moved(zyx, 0, away // 4), 1, away % 4)
        at = far[0] * 4 + far[1]
        return pltpu.make_async_remote_copy(
            src_ref=disp.at[at],
            dst_ref=stage1.at[at if incoming else me_g],
            send_sem=send1.at[g],
            recv_sem=recv1.at[g],
            device_id=device(far, tp),
            device_id_type=MESH,
        )

    for g in range(1, 16):
        first(g, False).start()
    stage1[me_g] = disp[me_g]
    gather.finish(1)
    for g in range(1, 16):
        first(g, True).wait_recv()
    o, i = iota((128, 128), 0), iota((128, 128), 1)
    turn = one_hot(i == ((o % 32) // 2) * 8 + (o // 32) * 2 + o % 2)
    turned[...] = dot(turn, stage1[...].reshape(128, 1408)).astype(BF16).reshape(4, 32, 1408)

    def second(g, incoming):
        far = moved(zyx, 2, -g if incoming else g)
        return pltpu.make_async_remote_copy(
            src_ref=turned.at[far[2]],
            dst_ref=stage2.at[far[2] if incoming else x],
            send_sem=send2.at[g],
            recv_sem=recv2.at[g],
            device_id=device(far, tp),
            device_id_type=MESH,
        )

    for g in range(1, 4):
        second(g, False).start()
    gather.start(2)
    stage2[x] = turned[x]
    for g in range(1, 4):
        second(g, True).wait_recv()

    arrived = stage2[...].reshape(128, 1408)
    rows_in = arrived[:, 0:1280]
    meta_in = arrived[:, 1280:1408].astype(F32)
    loads[8].wait()

    def swap(piece):
        cols = pl.ds(896 * piece, 896)
        return pltpu.make_async_remote_copy(
            src_ref=part_s.at[:, cols],
            dst_ref=part_r.at[:, cols],
            send_sem=send3.at[piece],
            recv_sem=recv3.at[piece],
            device_id=(seq, 1 - tp),
            device_id_type=MESH,
        )

    for piece in range(4):
        cols = slice(896 * piece, 896 * piece + 896)
        partial = dot(rows_in, down_v[:, cols])
        part_f[:, cols] = partial
        part_s[:, cols] = partial.astype(BF16)
        swap(piece).start()

    totals = jnp.sum(meta_in, axis=0, keepdims=True) * 0.5
    smaller = (doc_lane < doc_col) & (doc_lane >= 0.0)
    start_col = jnp.sum(jnp.where(smaller, totals, 0.0), axis=1, keepdims=True)
    start_out[...] = jnp.broadcast_to(start_col, (256, 128))

    slot_row = to_row(meta_in[:, 0:1])
    spot = (iota((256, 128), 0) + 1).astype(F32) == slot_row
    placed = one_hot(spot)
    hit = jnp.sum(jnp.where(spot, 1.0, 0.0), axis=1, keepdims=True) > 0.5
    loads[9].wait()
    squares = jnp.zeros((256, 1), F32)
    for piece in range(4):
        cols = slice(896 * piece, 896 * piece + 896)
        swap(piece).wait_recv()
        merged[...] = (part_f[:, cols] + part_r[:, cols].astype(F32)).astype(BF16)
        layer = jnp.where(hit, dot(placed, merged[...]), text_v[:, cols].astype(F32))
        text_v[:, cols] = layer.astype(BF16)
        squares += jnp.sum(layer * layer, axis=1, keepdims=True)
    out = pltpu.make_async_copy(
        text_v.at[:, pl.ds(pl.multiple_of(tp * 1792, 128), 1792)], layer_out, load.at[10]
    )
    out.start()
    gather.forward(2)
    factor = lax.rsqrt(squares * (1.0 / 3584.0) + EPS)
    for piece in range(4):
        cols = slice(896 * piece, 896 * piece + 896)
        normed[:, cols] = (text_v[:, cols].astype(F32) * factor).astype(BF16)

    pair = iota((256, 128), 1) % 64
    inverse = jnp.exp(pair.astype(F32) * (-2.0 / 128.0 * 13.815510557964274))
    at_t = to_column(positions[0:1, :].astype(F32))
    at_h = to_column(positions[1:2, :].astype(F32))
    at_w = to_column(positions[2:3, :].astype(F32))
    coord = jnp.where(pair < 16, at_t, jnp.where(pair < 40, at_h, at_w))
    angle = coord * inverse
    cosine = jnp.cos(angle)
    sine = jnp.sin(angle)
    sine = jnp.where(iota((256, 128), 1) < 64, -sine, sine)

    gather.finish(2)

    def rotated(v):
        return v * cosine + pltpu.roll(v, 64, 1) * sine

    for piece in range(3):
        w = weights[:, :, :, :, 384 * piece : 384 * piece + 384].reshape(3584, 384)
        qkv[...] = dot(normed[...], w)
        for head in range(3):
            v = qkv[:, 128 * head : 128 * head + 128]
            at = 3 * piece + head
            if at < 7:
                q_out[at] = rotated(v).astype(BF16)
            elif at == 7:
                kv_out[:, 0:128] = rotated(v).astype(BF16)
            else:
                kv_out[:, 128:256] = v.astype(BF16)

    out.wait()
    gather.drain()
    for g in range(1, 16):
        first(g, False).wait_send()
    for g in range(1, 4):
        second(g, False).wait_send()
    for piece in range(4):
        swap(piece).wait_send()


def back(q_ref, kv_ref, start_ref, out_ref, kv, q_v, acc, top, total, load, send, recv):
    zyx, tp, seq = coords()
    z, y, x = zyx
    mine = pltpu.make_async_copy(kv_ref, kv.at[z, y, x], load.at[0])
    mine.start()
    barrier = pltpu.get_barrier_semaphore()
    for dim in range(3):
        for by in (1, -1):
            pl.semaphore_signal(
                barrier, inc=1, device_id=device(moved(zyx, dim, by), tp), device_id_type=MESH
            )
    mine.wait()
    pl.semaphore_wait(barrier, 6)
    bounds = ((0, 96), (96, 80), (176, 80))

    def part_of(part, index):
        return kv.at[index + (pl.ds(*bounds[part]), slice(None))]

    gather = Gather(part_of, send, recv, zyx, tp)
    for phase in range(3):
        gather.start(phase)
        gather.forward(phase)
        gather.finish(phase)
    gather.drain()

    scale = HEAD**-0.5
    top[...] = jnp.full(top.shape, MASKED, F32)
    total[...] = jnp.zeros(total.shape, F32)
    acc[...] = jnp.zeros(acc.shape, F32)
    last = seq // 4
    count = last - jnp.maximum(seq - WINDOW, 0) // 4 + 1
    starts = start_ref[...][:, 0:1]

    def group(step, _):
        at = last - step
        gz, gy = at // 4, at % 4
        keys = kv[gz, gy, :, :, 0:128].reshape(1024, 128)
        values = kv[gz, gy, :, :, 128:256].reshape(1024, 128)
        key_pos = (iota((256, 1024), 1) + at * 1024).astype(F32)
        query_pos = (iota((256, 1024), 0) + seq * 256).astype(F32)
        allowed = (key_pos <= query_pos) & (key_pos >= starts)

        def head(h, _):
            scores = lax.dot_general(
                q_ref[h], keys, (((1,), (1,)), ((), ())), preferred_element_type=F32
            )
            scores = jnp.where(allowed, scores * scale, MASKED)
            old = top[h]
            new = jnp.maximum(old, jnp.max(scores, axis=1, keepdims=True))
            probs = jnp.exp(scores - new[:, 0:1])
            factor = jnp.exp(old - new)
            total[h] = total[h] * factor + jnp.sum(probs, axis=1, keepdims=True)
            acc[h] = acc[h] * factor + dot(probs.astype(BF16), values)
            top[h] = new
            return 0

        lax.fori_loop(0, 7, head, 0)
        return 0

    lax.fori_loop(0, count, group, 0)
    for h in range(7):
        out_ref[:, 128 * h : 128 * h + 128] = (acc[h] / total[h]).astype(BF16)


def per_device(
    patches, merge_up, merge_down, dest, slot, text, positions, documents, w_query, w_key, w_value
):
    hbm = pl.BlockSpec(memory_space=pl.ANY)
    vmem = pl.BlockSpec(memory_space=pltpu.VMEM)
    dma = pltpu.SemaphoreType.DMA
    layer_part, q, kv, starts = pl.pallas_call(
        front,
        out_shape=(
            jax.ShapeDtypeStruct((256, 1792), BF16),
            jax.ShapeDtypeStruct((7, 256, 128), BF16),
            jax.ShapeDtypeStruct((256, 256), BF16),
            jax.ShapeDtypeStruct((256, 128), F32),
        ),
        in_specs=[hbm, hbm, hbm, vmem, vmem, hbm, vmem, vmem, hbm, hbm, hbm],
        out_specs=(hbm, vmem, vmem, vmem),
        scratch_shapes=[
            pltpu.VMEM((256, 1280), BF16),
            pltpu.VMEM((4, 1280, 1280), BF16),
            pltpu.VMEM((1280, 3584), BF16),
            pltpu.VMEM((256, 3584), BF16),
            pltpu.VMEM((256, 1280), BF16),
            pltpu.VMEM((64, 1280), F32),
            pltpu.VMEM((16, 8, 1408), BF16),
            pltpu.VMEM((16, 8, 1408), BF16),
            pltpu.VMEM((4, 32, 1408), BF16),
            pltpu.VMEM((4, 32, 1408), BF16),
            pltpu.VMEM((128, 3584), F32),
            pltpu.VMEM((128, 3584), BF16),
            pltpu.VMEM((128, 3584), BF16),
            pltpu.VMEM((128, 896), BF16),
            pltpu.VMEM((256, 3584), BF16),
            pltpu.VMEM((4, 4, 4, 56, 1152), BF16),
            pltpu.VMEM((256, 384), F32),
            dma((11,)),
            dma((54,)),
            dma((54,)),
            dma((16,)),
            dma((16,)),
            dma((4,)),
            dma((4,)),
            dma((4,)),
            dma((4,)),
        ],
        compiler_params=pltpu.CompilerParams(
            collective_id=0, has_side_effects=True, vmem_limit_bytes=60 * 1024 * 1024
        ),
        name="front",
    )(
        patches, merge_up, merge_down, dest.reshape(1, -1), slot.reshape(1, -1), text, positions,
        documents.reshape(1, -1), w_query, w_key, w_value,
    )
    attended = pl.pallas_call(
        back,
        out_shape=jax.ShapeDtypeStruct((256, 896), BF16),
        in_specs=[vmem, hbm, vmem],
        out_specs=vmem,
        scratch_shapes=[
            pltpu.VMEM((4, 4, 4, 256, 256), BF16),
            pltpu.VMEM((7, 256, 128), BF16),
            pltpu.VMEM((7, 256, 128), F32),
            pltpu.VMEM((7, 256, 128), F32),
            pltpu.VMEM((7, 256, 128), F32),
            dma((1,)),
            dma((54,)),
            dma((54,)),
        ],
        compiler_params=pltpu.CompilerParams(
            collective_id=1, has_side_effects=True, vmem_limit_bytes=60 * 1024 * 1024
        ),
        name="back",
    )(q, kv, starts)
    return (layer_part, attended)


def solution(mesh):
    in_specs = (
        P("seq", None),
        P(None, "tp"),
        P("tp", None),
        P("seq"),
        P("seq"),
        P("seq", None),
        P(None, "seq"),
        P("seq"),
        P("seq", "tp"),
        P("seq", "tp"),
        P("seq", "tp"),
    )
    out_specs = (P("seq", "tp"), P("seq", "tp"))
    return jax.shard_map(
        per_device, mesh=mesh, in_specs=in_specs, out_specs=out_specs, check_vma=False
    )
```

time: 485 us -> 166 us (0.34)
  the two profiles are of different devices: /device:TPU:64 before, /device:TPU:96 now
where the time goes in v1:
time: 166 us
  Pallas kernels  161 us (97%)
  local copies, waits for them, and re-layouts  3.98 us (2%)
    pallas_call x1, Pallas kernels, per_device(): pl.pallas_call(back, out_shape=jax.ShapeDtypeStruct((256, 896), BF16), in...  105 us
    pallas_call x1, Pallas kernels, per_device(): pl.pallas_call(front, out_shape=(jax.ShapeDtypeStruct((256, 1792), BF16),...  56.1 us
    unnamed x2, local copies, waits for them, and re-layouts  3.98 us

profile of v1, /device:TPU:96, one launch (start us, length us, event | category | flops | bytes accessed | tf_op | source)
XLA Modules:
  0.0 166.0 jit_solution(5280781120813207617)
XLA Ops:
  0.6 56.1 %front.1 = (bf16[256,1792]{1,0:T(8,128)(2,1)}, bf16[7,256,128]{2,1,0:T(8,128)(2,1)}, bf16[256,256]{1,0:T(8,128)(2,1)}, f32[256,128]{1,0:T(8,128)}) custom-call(bf16[256,1280]{1,0:T(8,128)(2,1)} %patches.1, bf16[5120,1280]{1,0:T(8,128)(2,1)} %merge_up.1, bf16[1280,3584]{1,0:T(8,128)(2,1)} %merge_down.1, s32[1,64]{1,0:T(1,128)} %bitcast.4, s32[1,64]{1,0:T(1,128)} %bitcast.5, ...), custom_call_target="tpu_custom_call" | custom-call | tf_op jit(solution)/shard_map/front/pallas_call | solution.py:414
  56.7 105.2 %back.1 = bf16[256,896]{1,0:T(8,128)(2,1)} custom-call(bf16[7,256,128]{2,1,0:T(8,128)(2,1)} %get-tuple-element.7.q_ref, bf16[256,256]{1,0:T(8,128)(2,1)} %get-tuple-element.8.kv_ref, f32[256,128]{1,0:T(8,128)} %get-tuple-element.9.start_ref), custom_call_target="tpu_custom_call" | custom-call | tf_op jit(solution)/shard_map/back/pallas_call | solution.py:460
  162.0 2.2 %copy.15 = bf16[256,1792]{1,0:T(8,128)(2,1)} copy(bf16[256,1792]{1,0:T(8,128)(2,1)} %get-tuple-element.12) | data formatting | bytes 1835008
  164.1 1.8 %copy.16 = bf16[256,896]{1,0:T(8,128)(2,1)} copy(bf16[256,896]{1,0:T(8,128)(2,1)} %back.1) | data formatting | bytes 917504
